TPU v7x, 256 devices: a whole 4x4x8 slice. The times are simulated.
256 devices in a mesh: shard: 16 (over z, core), width: 4 (over x), shift: 4 (over y).
Axes of the slice: x: 4, y: 4, z: 8, core: 2. Of those that a mesh axis runs over, the one named last changes fastest.
Arguments:
- w_query: float32 [16384, 4096], P(('shift', 'shard'), 'width'), parts along dimension 0, may hold values from -0.125 to 0.125
- first_query: float32 [16384, 4096], P(('shift', 'shard'), 'width'), parts along dimension 0, may hold values from -0.09375 to 0.09375
- second_query: float32 [16384, 4096], P(('shift', 'shard'), 'width'), parts along dimension 0, may hold values from -0.09375 to 0.09375
- w_key: float32 [16384, 1024], P(('shift', 'shard'), 'width'), parts along dimension 0, may hold values from -0.125 to 0.125
- first_key: float32 [16384, 1024], P(('shift', 'shard'), 'width'), parts along dimension 0, may hold values from -0.09375 to 0.09375
- second_key: float32 [16384, 1024], P(('shift', 'shard'), 'width'), parts along dimension 0, may hold values from -0.09375 to 0.09375
- w_value: float32 [16384, 1024], P(('shift', 'shard'), 'width'), parts along dimension 0, may hold values from -0.125 to 0.125
- first_value: float32 [16384, 1024], P(('shift', 'shard'), 'width'), parts along dimension 0, may hold values from -0.09375 to 0.09375
- second_value: float32 [16384, 1024], P(('shift', 'shard'), 'width'), parts along dimension 0, may hold values from -0.09375 to 0.09375
- norm_gain: float32 [16384], P(('shift', 'shard')), parts along dimension 0, may hold values from 0.25 to 1.75
Outputs:
- ready_query: bfloat16 [16384, 4096], P('shift', 'width'), parts along dimension 0
- ready_key: bfloat16 [16384, 1024], P('shift', 'width'), parts along dimension 0
- ready_value: bfloat16 [16384, 1024], P('shift', 'width'), parts along dimension 0
- scale_query: float32 [16384], P(('shift', 'width')), parts along dimension 0
- scale_key: float32 [4096], P(('shift', 'width')), parts along dimension 0
- scale_value: float32 [4096], P(('shift', 'width')), parts along dimension 0
There are 4 independent parts, one for each index of `shift`. A program takes and returns all parts, laid end to end along the dimension named above; each array names one. Nothing has to cross between parts.
All inputs are finite; a program needn't handle non-finite values. Where the computation divides by a largest or mean magnitude, that divisor is 1e-20 or more.
Results may differ from a plain program's by a relative error of at most 0.001.
Values may be sent and summed in bfloat16 or wider, within the bound.
A program may use at most 128 MiB of HBM per device.

v0:
```python
import jax
import jax.numpy as jnp
from jax import lax
from jax.sharding import PartitionSpec as P

learn_rate = 0.25
hold_rate = 0.8


def sent_to_all(x, axis):
    length = lax.axis_size(axis)
    return lax.all_to_all(jnp.broadcast_to(x[None], (length, *x.shape)), axis, 0, 0, tiled=True)


def of_everyone(x, axis):
    everything = sent_to_all(x, axis)
    return jnp.max(everything, axis=0)


def in_one(arrays, axis):
    line, at, gathered = (jnp.concatenate([a.reshape(-1) for a in arrays]), 0, [])
    so_far = of_everyone(line, axis)
    for a in arrays:
        gathered.append(so_far[at : at + a.size].reshape(a.shape))
        at += a.size
    return tuple(gathered)


def side_by_side(arrays, axis, dim, along):
    ends, at = ([], 0)
    for a in arrays[:-1]:
        at += a.shape[along]
        ends.append(at)
    both = jnp.concatenate(arrays, axis=along)
    return tuple(jnp.split(lax.all_gather(both, axis, axis=dim, tiled=True), ends, axis=along))


def body(
    w_query,
    first_query,
    second_query,
    w_key,
    first_key,
    second_key,
    w_value,
    first_value,
    second_value,
    norm_gain,
):
    hold_query = hold_rate * first_query + second_query
    latest_query = w_query - learn_rate * hold_query
    hold_key = hold_rate * first_key + second_key
    latest_key = w_key - learn_rate * hold_key
    hold_value = hold_rate * first_value + second_value
    latest_value = w_value - learn_rate * hold_value
    latest_gained_query = latest_query * norm_gain[:, None]
    latest_gained_key = latest_key * norm_gain[:, None]
    latest_gained_value = latest_value * norm_gain[:, None]
    scale_query, scale_key, scale_value = in_one(
        (
            jnp.max(jnp.abs(latest_gained_query), axis=0),
            jnp.max(jnp.abs(latest_gained_key), axis=0),
            jnp.max(jnp.abs(latest_gained_value), axis=0),
        ),
        "shard",
    )
    narrow_query, narrow_key, narrow_value = (
        (latest_gained_query / scale_query).astype(jnp.bfloat16),
        (latest_gained_key / scale_key).astype(jnp.bfloat16),
        (latest_gained_value / scale_value).astype(jnp.bfloat16),
    )
    ready_query, ready_key, ready_value = side_by_side(
        (narrow_query, narrow_key, narrow_value), "shard", 0, 1
    )
    return (ready_query, ready_key, ready_value, scale_query, scale_key, scale_value)


def solution(mesh):
    in_specs = (
        P(("shift", "shard"), "width"),
        P(("shift", "shard"), "width"),
        P(("shift", "shard"), "width"),
        P(("shift", "shard"), "width"),
        P(("shift", "shard"), "width"),
        P(("shift", "shard"), "width"),
        P(("shift", "shard"), "width"),
        P(("shift", "shard"), "width"),
        P(("shift", "shard"), "width"),
        P(("shift", "shard")),
    )
    out_specs = (
        P("shift", "width"),
        P("shift", "width"),
        P("shift", "width"),
        P(("shift", "width")),
        P(("shift", "width")),
        P(("shift", "width")),
    )
    return jax.shard_map(body, mesh=mesh, in_specs=in_specs, out_specs=out_specs, check_vma=False)
```

profile of v0, /device:TPU:1, one launch (start us, length us, event | category | flops | bytes accessed | tf_op | source)
XLA Modules:
  0.0 120.9 jit_solution(3218607011323465067)
XLA Ops:
  7.2 0.0 copy-start.9
  7.2 0.0 copy-start.4
  7.2 0.0 copy-start.5
  7.2 0.0 copy-start.3
  7.2 0.0 copy-start.1
  7.2 0.0 copy-start.2
  7.2 0.0 copy-start
  7.2 0.0 all-gather.2.cloned.1.call-start
  7.3 2.2 %abs_reduce_fusion = (f32[1024]{0:T(1024)S(1)}, f32[256,1024]{1,0:T(8,128)S(1)}) fusion(f32[256]{0:T(256)} %param.19, f32[256,1024]{1,0:T(8,128)} %param.10, f32[256,1024]{1,0:T(8,128)} %param.12, f32[256,1024]{1,0:T(8,128)} %param.11), kind=kLoop, calls=%fused_computation.1 | loop fusion | flops 1833984 | bytes 4199424 | tf_op jit(solution)/shard_map/reduce_max | solution.py:61
  9.5 0.0 copy-done.9
  9.5 0.0 copy-done.4
  9.5 0.0 copy-done.5
  9.5 0.0 copy-done.3
  9.5 0.0 copy-done.1
  9.5 0.0 copy-done.2
  9.5 0.0 copy-done
  9.6 0.1 abs_reduce_fusion.2
  9.7 0.1 broadcast_in_dim.2
  9.8 18.2 %all_to_all.6 = f32[16,1,1536]{2,1,0:T(1,128)S(1)} all-to-all(f32[16,1,1536]{2,1,0:T(1,128)S(1)} %broadcast_in_dim.2), channel_id=1, replica_groups=mesh['shard'=16,'width'=4,'shift'=4] {'shard'}, dimensions={0} | all-to-all | bytes 196608 | tf_op jit(solution)/shard_map/all_to_all | solution.py:12
  28.0 0.1 reduce_max.39
  28.1 0.0 copy-start.7
  28.1 0.0 copy-start.8
  28.1 0.0 copy-start.6
  28.1 0.1 divide_convert_fusion
  28.3 0.9 pad_maximum_fusion
  29.2 0.0 all-gather.2.cloned.1.call-update
  29.2 0.0 copy-done.7
  29.2 0.0 copy-done.8
  29.3 0.0 copy-done.6
  29.3 72.6 %all-gather.2.cloned.1.call-done = bf16[4096,1536]{1,0:T(8,128)(2,1)} async-done(((bf16[256,1536]{1,0:T(8,128)(2,1)}), bf16[4096,1536]{1,0:T(8,128)(2,1)}) %all-gather.2.cloned.1.call-update) | async-done | bytes 12582928 | tf_op jit(solution)/shard_map/all_gather | solution.py:35
  101.8 4.5 %fusion = (bf16[4096,256]{1,0:T(8,128)(2,1)}, bf16[4096,256]{1,0:T(8,128)(2,1)}) fusion(bf16[4096,1536]{1,0:T(8,128)(2,1)} %all-gather.2.cloned.1.call-done), kind=kLoop, calls=%fused_computation.11 | loop fusion | bytes 8388608 | tf_op jit(solution)/shard_map/split | solution.py:35
  106.3 7.8 %split.12 = bf16[4096,1024]{1,0:T(8,128)(2,1)} slice(bf16[4096,1536]{1,0:T(8,128)(2,1)} %all-gather.2.cloned.1.call-done), slice={[0:4096], [0:1024]} | slice | bytes 16777216 | tf_op jit(solution)/shard_map/split | solution.py:35
  (4 shorter events, 0.1 us)
Async XLA Ops:
  7.2 2.3 %copy-start.9 = (f32[256]{0:T(256)S(1)}, f32[256]{0:T(256)}, u32[]{:S(2)}) copy-start(f32[256]{0:T(256)} %param.19) | copy-start | bytes 3076
  7.2 2.3 %copy-start.4 = (f32[256,256]{1,0:T(8,128)S(1)}, f32[256,256]{1,0:T(8,128)}, u32[]{:S(2)}) copy-start(f32[256,256]{1,0:T(8,128)} %param.18) | copy-start | bytes 786436
  7.2 2.3 %copy-start.5 = (f32[256,256]{1,0:T(8,128)S(1)}, f32[256,256]{1,0:T(8,128)}, u32[]{:S(2)}) copy-start(f32[256,256]{1,0:T(8,128)} %param.17) | copy-start | bytes 786436
  7.2 2.3 %copy-start.3 = (f32[256,256]{1,0:T(8,128)S(1)}, f32[256,256]{1,0:T(8,128)}, u32[]{:S(2)}) copy-start(f32[256,256]{1,0:T(8,128)} %param.16) | copy-start | bytes 786436
  7.2 2.3 %copy-start.1 = (f32[256,256]{1,0:T(8,128)S(1)}, f32[256,256]{1,0:T(8,128)}, u32[]{:S(2)}) copy-start(f32[256,256]{1,0:T(8,128)} %param.15) | copy-start | bytes 786436
  7.2 2.3 %copy-start.2 = (f32[256,256]{1,0:T(8,128)S(1)}, f32[256,256]{1,0:T(8,128)}, u32[]{:S(2)}) copy-start(f32[256,256]{1,0:T(8,128)} %param.14) | copy-start | bytes 786436
  7.2 2.3 %copy-start = (f32[256,256]{1,0:T(8,128)S(1)}, f32[256,256]{1,0:T(8,128)}, u32[]{:S(2)}) copy-start(f32[256,256]{1,0:T(8,128)} %param.13) | copy-start | bytes 786436
  7.2 94.6 %all-gather.2.cloned.1.call-start = ((), (), s32[]{:S(2)}) async-start(), calls=%async_computation.1 | async-start | bytes 13369344 | tf_op jit(solution)/shard_map/all_gather | solution.py:35
  28.1 1.2 copy-start.7
  28.1 1.2 copy-start.8
  28.1 1.1 copy-start.6
Sparse Core Ops, SparseCore 0:
  29.4 72.4 all-gather.1
where the time goes:
time: 121 us
  waiting for transfers between devices  72.6 us (60%)
  blocking collectives  18.2 us (15%)
  between operations  14.2 us (12%)
  local copies, waits for them, and re-layouts  12.4 us (10%)
  other arithmetic  3.48 us (3%)
    all_gather x1, waiting for transfers between devices, side_by_side(): lax.all_gather(both, axis, axis=dim, tiled=True)  72.6 us
    all_to_all x1, blocking collectives, sent_to_all(): lax.all_to_all(jnp.broadcast_to(x[None], (length, *x.shape)), axis, 0, 0,...  18.2 us
    split x2, local copies, waits for them, and re-layouts, side_by_side(): jnp.split(lax.all_gather(both, axis, axis=dim, tiled=True), ends, axis=al...  12.3 us
  transfers between devices with their start and end apart: 1, of which 1 were waited for; matrix products, arithmetic and copies ran while one was open for 0% of the time, Pallas kernels for 0%

commit v1 on v0

v1 whole, which is shorter than its diff:
```python
import jax
import jax.numpy as jnp
from jax import lax
from jax.experimental import pallas as pl
from jax.experimental.pallas import tpu as pltpu
from jax.sharding import PartitionSpec as P

learn_rate = 0.25
hold_rate = 0.8

MESH = pl.DeviceIdType.MESH
AXIS = "shard"
LOADS = 4
STRIP = 16


def make_kernel(n, rows, widths):
    rings = n // 2
    half = rows // 2
    load_rows = rows // LOADS
    starts = [sum(widths[:t]) for t in range(3)]
    total = sum(widths)
    pieces = ((0, 0, half), (0, half, half), (1, 0, rows), (2, 0, rows))
    far = rings // 2

    def kernel(*refs):
        ins = refs[:10]
        gathered, scales = refs[10:13], refs[13:16]
        bufs = refs[16:26]
        fresh, peaks = refs[26:28]
        load_sem, peak_send, peak_recv, ici_send, ici_recv, d2d_send, d2d_recv = refs[28:]

        me = lax.axis_index(AXIS)
        z, core = me // 2, me % 2
        partner = {AXIS: z * 2 + (1 - core)}

        barrier = pltpu.get_barrier_semaphore()
        for off in range(1, n):
            pl.semaphore_signal(
                barrier, inc=1, device_id={AXIS: lax.rem(me + off, n)}, device_id_type=MESH
            )

        def load(a, part):
            span = pl.ds(part * load_rows, load_rows)
            return pltpu.make_async_copy(
                ins[a].at[span, :], bufs[a].at[span, :], load_sem.at[part, a]
            )

        gain_copy = pltpu.make_async_copy(ins[9], bufs[9], load_sem.at[LOADS, 0])
        gain_copy.start()
        for part in range(LOADS):
            for a in range(9):
                load(a, part).start()
        gain_copy.wait()

        tall = jnp.transpose(jnp.broadcast_to(bufs[9][...], (128, rows)))

        tops = [jnp.zeros((8, w), jnp.float32) for w in widths]
        for part in range(LOADS):
            for a in range(9):
                load(a, part).wait()
            for r in range(part * load_rows, (part + 1) * load_rows, 8):
                for t in range(3):
                    w, first, second = (bufs[3 * t + k][r : r + 8, :] for k in range(3))
                    hold = hold_rate * first + second
                    latest = w - learn_rate * hold
                    gain = jnp.concatenate([tall[r : r + 8, :]] * (widths[t] // 128), axis=1)
                    gained = latest * gain
                    fresh[r : r + 8, starts[t] : starts[t] + widths[t]] = gained
                    tops[t] = jnp.maximum(tops[t], jnp.abs(gained))
        for t in range(3):
            peaks[me, :, starts[t] : starts[t] + widths[t]] = jnp.max(tops[t], axis=0, keepdims=True)

        pl.semaphore_wait(barrier, n - 1)

        def tell(off):
            return pltpu.make_async_remote_copy(
                src_ref=peaks.at[me],
                dst_ref=peaks.at[me],
                send_sem=peak_send.at[off],
                recv_sem=peak_recv.at[off],
                device_id={AXIS: lax.rem(me + off, n)},
                device_id_type=MESH,
            )

        def hear(off):
            source = lax.rem(me + n - off, n)
            return pltpu.make_async_remote_copy(
                src_ref=peaks.at[source],
                dst_ref=peaks.at[source],
                send_sem=peak_send.at[off],
                recv_sem=peak_recv.at[off],
                device_id={AXIS: source},
                device_id_type=MESH,
            )

        order = sorted(range(1, n), key=lambda off: -min(off, n - off))
        for off in order:
            tell(off).start()
        for off in range(1, n):
            hear(off).wait_recv()
        top = jnp.max(peaks[...], axis=0)
        for t in range(3):
            scales[t][...] = top[:, starts[t] : starts[t] + widths[t]]

        def at(block, which, p):
            t, first, count = pieces[p]
            return gathered[t].at[pl.ds((block * 2 + which) * rows + first, count), :]

        def ring(step, p, way):
            block = lax.rem(z + rings - step if way == 0 else z + step, rings)
            target = lax.rem(z + 1 if way == 0 else z + rings - 1, rings)
            return pltpu.make_async_remote_copy(
                src_ref=at(block, core, p),
                dst_ref=at(block, core, p),
                send_sem=ici_send.at[way, step, p],
                recv_sem=ici_recv.at[way, step, p],
                device_id={AXIS: target * 2 + core},
                device_id_type=MESH,
            )

        def arrival(step, p, way):
            block = lax.rem(z + rings - 1 - step if way == 0 else z + 1 + step, rings)
            target = lax.rem(z + 1 if way == 0 else z + rings - 1, rings)
            return pltpu.make_async_remote_copy(
                src_ref=at(block, core, p),
                dst_ref=at(block, core, p),
                send_sem=ici_send.at[way, step, p],
                recv_sem=ici_recv.at[way, step, p],
                device_id={AXIS: target * 2 + core},
                device_id_type=MESH,
            )

        def across(block, slot, p, which):
            return pltpu.make_async_remote_copy(
                src_ref=at(block, which, p),
                dst_ref=at(block, which, p),
                send_sem=d2d_send.at[slot, p],
                recv_sem=d2d_recv.at[slot, p],
                device_id=partner,
                device_id_type=MESH,
            )

        def carried(step, p, way):
            return step < far - 1 or p % 2 == way

        sent, crossed = [], []

        def pass_on(step, p, way):
            copy = ring(step, p, way)
            copy.start()
            sent.append(copy)

        def cross(block, slot, p):
            across(block, slot, p, core).start()
            crossed.append((block, slot, p))

        inv = 1.0 / top
        for p, (t, first, count) in enumerate(pieces):
            for r in range(first, first + count, STRIP):
                row = pl.multiple_of(me * rows + r, STRIP)
                value = fresh[r : r + STRIP, starts[t] : starts[t] + widths[t]]
                value = value * inv[:, starts[t] : starts[t] + widths[t]]
                gathered[t][pl.ds(row, STRIP), :] = value.astype(jnp.bfloat16)
        for p in range(4):
            pass_on(0, p, 0)
            pass_on(0, p, 1)
        for p in range(4):
            cross(z, 0, p)

        for step in range(far):
            for p in range(4):
                for way in range(2):
                    if not carried(step, p, way):
                        continue
                    arrival(step, p, way).wait_recv()
                    if step + 1 < far and carried(step + 1, p, way):
                        pass_on(step + 1, p, way)
                    distance = step + 1
                    slot = distance if way == 0 or distance == far else rings - distance
                    block = lax.rem(z + rings - distance if way == 0 else z + distance, rings)
                    cross(block, slot, p)

        for block, slot, p in crossed:
            across(block, slot, p, 1 - core).wait_recv()
        for copy in sent:
            copy.wait_send()
        for block, slot, p in crossed:
            across(block, slot, p, core).wait_send()
        for off in range(1, n):
            tell(off).wait_send()

    out_shape = tuple(pltpu.VMEM((n * rows, w), jnp.bfloat16) for w in widths) + tuple(
        pltpu.VMEM((1, w), jnp.float32) for w in widths
    )
    vmem = pl.BlockSpec(memory_space=pltpu.VMEM)
    return pl.pallas_call(
        kernel,
        name="update_gather",
        out_shape=out_shape,
        in_specs=[pl.BlockSpec(memory_space=pltpu.HBM)] * 10,
        out_specs=(vmem,) * 6,
        scratch_shapes=[pltpu.VMEM((rows, w), jnp.float32) for w in widths for _ in range(3)]
        + [
            pltpu.VMEM((1, rows), jnp.float32),
            pltpu.VMEM((rows, total), jnp.float32),
            pltpu.VMEM((n, 1, total), jnp.float32),
            pltpu.SemaphoreType.DMA((LOADS + 1, 9)),
            pltpu.SemaphoreType.DMA((n,)),
            pltpu.SemaphoreType.DMA((n,)),
            pltpu.SemaphoreType.DMA((2, far, 4)),
            pltpu.SemaphoreType.DMA((2, far, 4)),
            pltpu.SemaphoreType.DMA((rings, 4)),
            pltpu.SemaphoreType.DMA((rings, 4)),
        ],
        compiler_params=pltpu.CompilerParams(
            collective_id=0, has_side_effects=True, vmem_limit_bytes=40 * 1024 * 1024
        ),
    )


def body(
    w_query,
    first_query,
    second_query,
    w_key,
    first_key,
    second_key,
    w_value,
    first_value,
    second_value,
    norm_gain,
):
    n = lax.axis_size(AXIS)
    rows = w_query.shape[0]
    widths = (w_query.shape[1], w_key.shape[1], w_value.shape[1])
    call = make_kernel(n, rows, widths)
    large = (
        w_query,
        first_query,
        second_query,
        w_key,
        first_key,
        second_key,
        w_value,
        first_value,
        second_value,
        norm_gain.reshape(1, rows),
    )
    large = [pltpu.with_memory_space_constraint(a, pltpu.HBM) for a in large]
    outs = call(*large)
    return tuple(outs[:3]) + tuple(s.reshape(-1) for s in outs[3:])


def solution(mesh):
    by_row = P(("shift", "shard"), "width")
    in_specs = (by_row,) * 9 + (P(("shift", "shard")),)
    out_specs = (P("shift", "width"),) * 3 + (P(("shift", "width")),) * 3
    return jax.shard_map(body, mesh=mesh, in_specs=in_specs, out_specs=out_specs, check_vma=False)
```

time: 121 us -> 87 us (0.72)
  Pallas kernels: 0 us -> 78.5 us
  waiting for transfers between devices: 72.6 us -> 0 us
  blocking collectives: 18.2 us -> 0 us
  between operations: 14.2 us -> 0.65 us
  local copies, waits for them, and re-layouts: 12.4 us -> 7.75 us
  other arithmetic: 3.48 us -> 0 us
    pallas_call x0 -> x1, Pallas kernels: none -> 78.5 us  [body(): outs = call(*large)]
    all_gather x1 -> x0, waiting for transfers between devices: 72.6 us -> none  [side_by_side(): lax.all_gather(both, axis, axis=dim, tiled=True)]
    all_to_all x1 -> x0, blocking collectives: 18.2 us -> none  [sent_to_all(): lax.all_to_all(jnp.broadcast_to(x[None], (length, *x.shape)), axis, 0, 0,...]
    split x2 -> x0, local copies, waits for them, and re-layouts: 12.3 us -> none  [side_by_side(): jnp.split(lax.all_gather(both, axis, axis=dim, tiled=True), ends, axis=al...]
    unnamed x20 -> x6, local copies, waits for them, and re-layouts: 0.05 us -> 7.75 us
    reduce_max x3 -> x0, other arithmetic: 2.4 us -> none  [the longest x1 2.2 us: body(): jnp.max(jnp.abs(latest_gained_query), axis=0)]
  transfers between devices with their start and end apart: 1 -> 0, of which waited for: 1 -> 0; matrix products, arithmetic and copies ran while one was open for 0% -> 0% of each run, Pallas kernels for 0% -> 0%
where the time goes in v1:
time: 87 us; the launch traced here: 86.9 us
  Pallas kernels  78.5 us (90%)
  local copies, waits for them, and re-layouts  7.75 us (9%)
    pallas_call x1, Pallas kernels, body(): outs = call(*large)  78.5 us
    unnamed x6, local copies, waits for them, and re-layouts  7.75 us

profile of v1, /device:TPU:1, one launch (start us, length us, event | category | flops | bytes accessed | tf_op | source)
XLA Modules:
  0.0 86.9 jit_solution(3543906188107678485)
XLA Ops:
  0.6 78.5 %update_gather.1 = (bf16[4096,1024]{1,0:T(8,128)(2,1)S(1)}, bf16[4096,256]{1,0:T(8,128)(2,1)S(1)}, bf16[4096,256]{1,0:T(8,128)(2,1)S(1)}, f32[1,1024]{1,0:T(1,12...) custom-call(f32[256,1024]{1,0:T(8,128)} %refs_0_.1, f32[256,1024]{1,0:T(8,128)} %refs_1_.1, f32[256,1024]{1,0:T(8,128)} %refs_2_.1, ...), custom_call_target="tpu_custom_call" | custom-call | tf_op jit(solution)/shard_map/update_gather/pallas_call | solution.py:251
  79.2 3.4 %copy.22 = bf16[4096,1024]{1,0:T(8,128)(2,1)} copy(bf16[4096,1024]{1,0:T(8,128)(2,1)S(1)} %get-tuple-element.18) | data formatting | bytes 16777216
  82.6 0.6 copy.26
  83.1 0.6 copy.27
  83.7 0.6 copy.25
  84.3 1.3 %copy.23 = bf16[4096,256]{1,0:T(8,128)(2,1)} copy(bf16[4096,256]{1,0:T(8,128)(2,1)S(1)} %get-tuple-element.19) | data formatting | bytes 4194304
  85.6 1.3 %copy.24 = bf16[4096,256]{1,0:T(8,128)(2,1)} copy(bf16[4096,256]{1,0:T(8,128)(2,1)S(1)} %get-tuple-element.20) | data formatting | bytes 4194304

commit v2 on v1

v2 whole, which is shorter than its diff:
```python
import jax
import jax.numpy as jnp
from jax import lax
from jax.experimental import pallas as pl
from jax.experimental.pallas import tpu as pltpu
from jax.sharding import PartitionSpec as P

learn_rate = 0.25
hold_rate = 0.8

MESH = pl.DeviceIdType.MESH
AXIS = "shard"
LOADS = 4
STRIP = 16
EARLY = 32
CUT = 64
FAR_CUTS = ((64, 48, 16), (64, 48, 16))


def make_kernel(n, rows, widths):
    rings = n // 2
    far = rings // 2
    load_rows = rows // LOADS
    starts = [sum(widths[:t]) for t in range(3)]
    total = sum(widths)
    whole = tuple((first, CUT) for first in range(0, rows, CUT))
    assert sum(map(sum, FAR_CUTS)) == rows

    def last_pieces(way):
        first, out = way * sum(FAR_CUTS[0]), []
        for count in FAR_CUTS[way]:
            out.append((first, count))
            first += count
        return tuple(out)

    def carried(step, way):
        if step == far - 1:
            return last_pieces(way)
        if step == 0 and EARLY:
            return ((EARLY, CUT - EARLY),) + whole[1:]
        return whole

    slots, slot_of = 0, {}
    for way in range(2):
        for step in range(far):
            for p in range(len(carried(step, way))):
                slot_of[way, step, p] = slots
                slots += 1

    def kernel(*refs):
        ins = refs[:10]
        gathered, scales = refs[10], refs[11:14]
        land, gains, fresh, peaks, early = refs[14:19]
        load_sem, one_sem, ici_recv = refs[19:]
        gain_sem, peak_send, peak_recv, ici_send, d2d_send, d2d_recv, early_send = (
            one_sem.at[i] for i in range(7)
        )

        me = lax.axis_index(AXIS)
        z, core = me // 2, me % 2
        partner = {AXIS: z * 2 + (1 - core)}
        ahead = (lax.rem(z + 1, rings), lax.rem(z + rings - 1, rings))

        barrier = pltpu.get_barrier_semaphore()
        for off in range(1, n):
            pl.semaphore_signal(
                barrier, inc=1, device_id={AXIS: lax.rem(me + off, n)}, device_id_type=MESH
            )

        gain_copy = pltpu.make_async_copy(ins[9], gains, gain_sem)
        gain_copy.start()
        place, at = [], 0
        for t in range(3):
            for _ in range(3):
                place.append((at, widths[t]))
                at += widths[t]
        for part in range(LOADS):
            span = pl.ds(part * load_rows, load_rows)
            for a, (first, width) in enumerate(place):
                pltpu.make_async_copy(
                    ins[a].at[span, :],
                    land.at[span, pl.ds(first, width)],
                    load_sem.at[part],
                ).start()

        gain_copy.wait()
        tall = jnp.transpose(jnp.broadcast_to(gains[...], (128, rows)))
        tops = [jnp.zeros((8, w), jnp.float32) for w in widths]
        for part in range(LOADS):
            span = pl.ds(part * load_rows, load_rows)
            pltpu.make_async_copy(land.at[span, :], land.at[span, :], load_sem.at[part]).wait()
            for r in range(part * load_rows, (part + 1) * load_rows, 8):
                for t in range(3):
                    w, first, second = (
                        land[r : r + 8, place[3 * t + k][0] : place[3 * t + k][0] + widths[t]]
                        for k in range(3)
                    )
                    hold = hold_rate * first + second
                    latest = w - learn_rate * hold
                    gain = jnp.concatenate([tall[r : r + 8, :]] * (widths[t] // 128), axis=1)
                    gained = latest * gain
                    fresh[r : r + 8, starts[t] : starts[t] + widths[t]] = gained
                    tops[t] = jnp.maximum(tops[t], jnp.abs(gained))
        for t in range(3):
            peaks[me, :, starts[t] : starts[t] + widths[t]] = jnp.max(tops[t], axis=0, keepdims=True)

        pl.semaphore_wait(barrier, n - 1)

        for off in sorted(range(1, n), key=lambda off: -min(off, n - off)):
            pltpu.make_async_remote_copy(
                src_ref=peaks.at[me],
                dst_ref=peaks.at[me],
                send_sem=peak_send,
                recv_sem=peak_recv,
                device_id={AXIS: lax.rem(me + off, n)},
                device_id_type=MESH,
            ).start()

        def early_copy(way):
            return pltpu.make_async_remote_copy(
                src_ref=fresh.at[pl.ds(0, EARLY), :],
                dst_ref=early.at[way],
                send_sem=early_send,
                recv_sem=one_sem.at[7 + way],
                device_id={AXIS: ahead[way] * 2 + core},
                device_id_type=MESH,
            )

        if EARLY:
            for way in range(2):
                early_copy(way).start()

        others = peaks.at[pl.ds(0, n - 1)]
        pltpu.make_async_copy(others, others, peak_recv).wait()
        top = jnp.max(peaks[...], axis=0)
        inv = 1.0 / top

        def block_at(distance, way):
            if distance == 0:
                return z
            return lax.rem(z + rings - distance if way == 0 else z + distance, rings)

        def rows_of(block, first, count):
            return gathered.at[pl.ds(me_rows(block) + first, count), :]

        def me_rows(block):
            return pl.multiple_of((block * 2 + core) * rows, STRIP)

        def hop(block, way, step, p):
            first, count = carried(step, way)[p]
            return pltpu.make_async_remote_copy(
                src_ref=rows_of(block, first, count),
                dst_ref=rows_of(block, first, count),
                send_sem=ici_send,
                recv_sem=ici_recv.at[slot_of[way, step, p]],
                device_id={AXIS: ahead[way] * 2 + core},
                device_id_type=MESH,
            )

        def cross(block, first, count):
            pltpu.make_async_remote_copy(
                src_ref=rows_of(block, first, count),
                dst_ref=rows_of(block, first, count),
                send_sem=d2d_send,
                recv_sem=d2d_recv,
                device_id=partner,
                device_id_type=MESH,
            ).start()

        def settle(source, base, first, count):
            for r in range(0, count, STRIP):
                row = pl.multiple_of(base + first + r, STRIP)
                gathered[pl.ds(row, STRIP), :] = (source(r) * inv).astype(jnp.bfloat16)

        if EARLY:
            settle(lambda r: fresh[r : r + STRIP, :], me_rows(z), 0, EARLY)
        settle(lambda r: fresh[EARLY + r : EARLY + r + STRIP, :], me_rows(z), EARLY, rows - EARLY)
        for p in range(len(whole)):
            for way in range(2):
                hop(z, way, 0, p).start()
        for first, count in whole:
            cross(z, first, count)
        for t in range(3):
            scales[t][...] = top[:, starts[t] : starts[t] + widths[t]]

        if EARLY:
            for way in range(2):
                early_copy(way).wait_recv()
                settle(lambda r: early[way, r : r + STRIP, :], me_rows(block_at(1, way)), 0, EARLY)

        for step in range(far):
            for p in range(max(len(carried(step, way)) for way in range(2))):
                for way in range(2):
                    if p >= len(carried(step, way)):
                        continue
                    block = block_at(step + 1, way)
                    hop(block, way, step, p).wait_recv()
                    first, count = carried(step, way)[p]
                    if step == 0 and p == 0:
                        first, count = 0, CUT
                    if step + 2 < far:
                        hop(block, way, step + 1, p).start()
                    elif step + 2 == far:
                        for q, (start, some) in enumerate(last_pieces(way)):
                            if first < start + some <= first + count:
                                hop(block, way, step + 1, q).start()
                    cross(block, first, count)

        def drain(sem, count):
            some = gathered.at[pl.ds(0, count), :]
            pltpu.make_async_copy(some, some, sem).wait()

        drain(d2d_recv, rings * rows)
        drain(ici_send, (rings - 1) * rows - 2 * EARLY)
        drain(d2d_send, rings * rows)
        pltpu.make_async_copy(others, others, peak_send).wait()
        if EARLY:
            pltpu.make_async_copy(early, early, early_send).wait()

    out_shape = (pltpu.VMEM((n * rows, total), jnp.bfloat16),) + tuple(
        pltpu.VMEM((1, w), jnp.float32) for w in widths
    )
    return pl.pallas_call(
        kernel,
        name="update_gather",
        out_shape=out_shape,
        in_specs=[pl.BlockSpec(memory_space=pltpu.HBM)] * 10,
        out_specs=(pl.BlockSpec(memory_space=pltpu.VMEM),) * 4,
        scratch_shapes=[
            pltpu.VMEM((rows, 3 * total), jnp.float32),
            pltpu.VMEM((1, rows), jnp.float32),
            pltpu.VMEM((rows, total), jnp.float32),
            pltpu.VMEM((n, 1, total), jnp.float32),
            pltpu.VMEM((2, max(EARLY, 8), total), jnp.float32),
            pltpu.SemaphoreType.DMA((LOADS,)),
            pltpu.SemaphoreType.DMA((9,)),
            pltpu.SemaphoreType.DMA((slots,)),
        ],
        compiler_params=pltpu.CompilerParams(
            collective_id=0, has_side_effects=True, vmem_limit_bytes=40 * 1024 * 1024
        ),
    )


def put_out(gathered, *refs):
    scales, outs, sems = refs[:3], refs[3:9], refs[9]
    rows, at, copies = gathered.shape[0], 0, []
    for t in range(3):
        width = outs[t].shape[1]
        cuts = 4 if t == 0 else 1
        for first in range(0, rows, rows // cuts):
            span = pl.ds(first, rows // cuts)
            pltpu.make_async_copy(
                gathered.at[span, pl.ds(at, width)], outs[t].at[span, :], sems.at[t]
            ).start()
        copies.append(
            pltpu.make_async_copy(gathered.at[:, pl.ds(at, width)], outs[t], sems.at[t])
        )
        at += width
    for t in range(3):
        copies.append(pltpu.make_async_copy(scales[t], outs[3 + t], sems.at[3 + t]))
        copies[-1].start()
    for copy in copies:
        copy.wait()


def body(
    w_query,
    first_query,
    second_query,
    w_key,
    first_key,
    second_key,
    w_value,
    first_value,
    second_value,
    norm_gain,
):
    n = lax.axis_size(AXIS)
    rows = w_query.shape[0]
    widths = (w_query.shape[1], w_key.shape[1], w_value.shape[1])
    ins = (
        w_query,
        first_query,
        second_query,
        w_key,
        first_key,
        second_key,
        w_value,
        first_value,
        second_value,
        norm_gain.reshape(1, rows),
    )
    ins = [pltpu.with_memory_space_constraint(a, pltpu.HBM) for a in ins]
    held = make_kernel(n, rows, widths)(*ins)
    outs = pl.pallas_call(
        put_out,
        name="put_out",
        out_shape=tuple(jax.ShapeDtypeStruct((n * rows, w), jnp.bfloat16) for w in widths)
        + tuple(jax.ShapeDtypeStruct((1, w), jnp.float32) for w in widths),
        in_specs=[pl.BlockSpec(memory_space=pltpu.VMEM)] * 4,
        out_specs=(pl.BlockSpec(memory_space=pltpu.HBM),) * 6,
        scratch_shapes=[pltpu.SemaphoreType.DMA((6,))],
        compiler_params=pltpu.CompilerParams(vmem_limit_bytes=16 * 1024 * 1024),
    )(*[pltpu.with_memory_space_constraint(a, pltpu.VMEM) for a in held])
    return tuple(outs[:3]) + tuple(s.reshape(-1) for s in outs[3:])


def solution(mesh):
    by_row = P(("shift", "shard"), "width")
    in_specs = (by_row,) * 9 + (P(("shift", "shard")),)
    out_specs = (P("shift", "width"),) * 3 + (P(("shift", "width")),) * 3
    return jax.shard_map(body, mesh=mesh, in_specs=in_specs, out_specs=out_specs, check_vma=False)
```

time: 87 us -> 80.7 us (0.928)
  local copies, waits for them, and re-layouts: 7.75 us -> 0 us
  Pallas kernels: 78.5 us -> 80 us
    unnamed x6 -> x0, local copies, waits for them, and re-layouts: 7.75 us -> none
    pallas_call x1 -> x2, Pallas kernels: 78.5 us -> 80 us  [the longest x1 75.3 us: body(): held = make_kernel(n, rows, widths)(*ins)]
where the time goes in v2:
time: 80.7 us; the launch traced here: 80.6 us
  Pallas kernels  80 us (99%)
    pallas_call x1, Pallas kernels, body(): held = make_kernel(n, rows, widths)(*ins)  75.3 us
    pallas_call x1, Pallas kernels, body(): pl.pallas_call(put_out, name='put_out', out_shape=tuple((jax.ShapeDtypeSt...  4.65 us

profile of v2, /device:TPU:1, one launch (start us, length us, event | category | flops | bytes accessed | tf_op | source)
XLA Modules:
  0.0 80.6 jit_solution(1172079203017555505)
XLA Ops:
  0.6 75.3 %update_gather.1 = (bf16[4096,1536]{1,0:T(8,128)(2,1)S(1)}, f32[1,1024]{1,0:T(1,128)S(1)}, f32[1,256]{1,0:T(1,128)S(1)}, f32[1,256]{1,0:T(1,128)S(1)}) custom-call(f32[256,1024]{1,0:T(8,128)} %refs_0_.1, f32[256,1024]{1,0:T(8,128)} %refs_1_.1, f32[256,1024]{1,0:T(8,128)} %refs_2_.1, f32[256,256]{1,0:T(8,128)} %refs_3_.1, f32[256,256]{1,0:T(8,128)} %refs_4_.1, ...), custom_call_target="tpu_custom_call" | custom-call | tf_op jit(solution)/shard_map/update_gather/pallas_call | solution.py:295
  76.0 4.7 %put_out.1 = (bf16[4096,1024]{1,0:T(8,128)(2,1)}, bf16[4096,256]{1,0:T(8,128)(2,1)}, bf16[4096,256]{1,0:T(8,128)(2,1)}, f32[1,1024]{1,0:T(1,128)}, f32[1,256]{1,0:T(1,128)}, /*index=5*/f32[1,256]{1,0:T(1,128)}) custom-call(bf16[4096,1536]{1,0:T(8,128)(2,1)S(1)} %get-tuple-element.16.gathered, f32[1,1024]{1,0:T(1,128)S(1)} %get-tuple-element.17.refs_0_, ...), custom_call_target="tpu_custom_call" | custom-call | tf_op jit(solution)/shard_map/put_out/pallas_call | solution.py:296

commit v3 on v2

--- a/solution.py
+++ b/solution.py
@@ -1,3 +1,5 @@
+import functools
+
 import jax
 import jax.numpy as jnp
 from jax import lax
@@ -15,6 +17,7 @@
 EARLY = 32
 CUT = 64
 FAR_CUTS = ((64, 48, 16), (64, 48, 16))
+LENT = 24
 
 
 def make_kernel(n, rows, widths):
@@ -26,16 +29,21 @@
     whole = tuple((first, CUT) for first in range(0, rows, CUT))
     assert sum(map(sum, FAR_CUTS)) == rows
 
-    def last_pieces(way):
+    def last_pieces(way, side):
         first, out = way * sum(FAR_CUTS[0]), []
-        for count in FAR_CUTS[way]:
+        for i, count in enumerate(FAR_CUTS[way]):
+            if LENT and side == 0 and i == 1:
+                count -= LENT
             out.append((first, count))
             first += count
         return tuple(out)
 
-    def carried(step, way):
+    def lent_rows(way):
+        return (way * sum(FAR_CUTS[0]) + sum(FAR_CUTS[way]) - LENT, LENT)
+
+    def carried(step, way, side):
         if step == far - 1:
-            return last_pieces(way)
+            return last_pieces(way, side)
         if step == 0 and EARLY:
             return ((EARLY, CUT - EARLY),) + whole[1:]
         return whole
@@ -43,7 +51,7 @@
     slots, slot_of = 0, {}
     for way in range(2):
         for step in range(far):
-            for p in range(len(carried(step, way))):
+            for p in range(len(carried(step, way, 0))):
                 slot_of[way, step, p] = slots
                 slots += 1
 
@@ -55,6 +63,8 @@
         gain_sem, peak_send, peak_recv, ici_send, d2d_send, d2d_recv, early_send = (
             one_sem.at[i] for i in range(7)
         )
+        lent_recv = [one_sem.at[9 + way] for way in range(2)]
+        lent_cross = [one_sem.at[11 + way] for way in range(2)]
 
         me = lax.axis_index(AXIS)
         z, core = me // 2, me % 2
@@ -140,32 +150,42 @@
                 return z
             return lax.rem(z + rings - distance if way == 0 else z + distance, rings)
 
-        def rows_of(block, first, count):
-            return gathered.at[pl.ds(me_rows(block) + first, count), :]
-
-        def me_rows(block):
-            return pl.multiple_of((block * 2 + core) * rows, STRIP)
-
-        def hop(block, way, step, p):
-            first, count = carried(step, way)[p]
+        def me_rows(block, side=core):
+            return pl.multiple_of((block * 2 + side) * rows, STRIP)
+
+        def rows_of(block, first, count, side=core):
+            return gathered.at[pl.ds(me_rows(block, side) + first, count), :]
+
+        def carry(block, way, first, count, recv_sem, side=core, to=core):
             return pltpu.make_async_remote_copy(
-                src_ref=rows_of(block, first, count),
-                dst_ref=rows_of(block, first, count),
+                src_ref=rows_of(block, first, count, side),
+                dst_ref=rows_of(block, first, count, side),
                 send_sem=ici_send,
-                recv_sem=ici_recv.at[slot_of[way, step, p]],
-                device_id={AXIS: ahead[way] * 2 + core},
+                recv_sem=recv_sem,
+                device_id={AXIS: ahead[way] * 2 + to},
                 device_id_type=MESH,
             )
 
-        def cross(block, first, count):
-            pltpu.make_async_remote_copy(
-                src_ref=rows_of(block, first, count),
-                dst_ref=rows_of(block, first, count),
+        def hop(block, way, step, p, side=0):
+            first, count = carried(step, way, side)[p]
+            return carry(block, way, first, count, ici_recv.at[slot_of[way, step, p]])
+
+        def across(block, first, count, side=core, recv_sem=d2d_recv):
+            return pltpu.make_async_remote_copy(
+                src_ref=rows_of(block, first, count, side),
+                dst_ref=rows_of(block, first, count, side),
                 send_sem=d2d_send,
-                recv_sem=d2d_recv,
+                recv_sem=recv_sem,
                 device_id=partner,
                 device_id_type=MESH,
-            ).start()
+            )
+
+        def cross(block, first, count):
+            across(block, first, count).start()
+
+        def each_side(run):
+            for side in range(2):
+                pl.when(core == side)(functools.partial(run, side))
 
         def settle(source, base, first, count):
             for r in range(0, count, STRIP):
@@ -188,31 +208,75 @@
                 early_copy(way).wait_recv()
                 settle(lambda r: early[way, r : r + STRIP, :], me_rows(block_at(1, way)), 0, EARLY)
 
+        def last_sent(way, p):
+            first, count = whole[p]
+            return [
+                q
+                for q, (start, some) in enumerate(last_pieces(way, 1))
+                if first < start + some <= first + count
+            ]
+
+        def holds_lent(way, p):
+            first, count = whole[p]
+            start, some = lent_rows(way)
+            return LENT and first <= start and start + some <= first + count
+
+        def onward(block, way, step, p, side):
+            for q in last_sent(way, p):
+                hop(block, way, step + 1, q, side).start()
+            first, count = whole[p]
+            if side == 0 and holds_lent(way, p):
+                across(block, first, count, recv_sem=lent_cross[way]).start()
+            else:
+                cross(block, first, count)
+
+        def lend(block, way, p):
+            first, count = whole[p]
+            across(block, first, count, side=0, recv_sem=lent_cross[way]).wait_recv()
+            start, some = lent_rows(way)
+            for to in range(2):
+                carry(block, way, start, some, lent_recv[way], side=0, to=to).start()
+
+        def arrive(block, way, step, p, side):
+            hop(block, way, step, p, side).wait_recv()
+            cross(block, *carried(step, way, side)[p])
+
+        def lent_arrive(block, way):
+            start, some = lent_rows(way)
+            carry(block, way, start, some, lent_recv[way], side=0, to=1).wait_recv()
+
         for step in range(far):
-            for p in range(max(len(carried(step, way)) for way in range(2))):
+            for p in range(len(carried(step, 0, 0))):
                 for way in range(2):
-                    if p >= len(carried(step, way)):
+                    block = block_at(step + 1, way)
+                    if step == far - 1:
+                        each_side(functools.partial(arrive, block, way, step, p))
                         continue
-                    block = block_at(step + 1, way)
                     hop(block, way, step, p).wait_recv()
-                    first, count = carried(step, way)[p]
-                    if step == 0 and p == 0:
-                        first, count = 0, CUT
-                    if step + 2 < far:
-                        hop(block, way, step + 1, p).start()
-                    elif step + 2 == far:
-                        for q, (start, some) in enumerate(last_pieces(way)):
-                            if first < start + some <= first + count:
-                                hop(block, way, step + 1, q).start()
-                    cross(block, first, count)
+                    if step == far - 2:
+                        each_side(functools.partial(onward, block, way, step, p))
+                        continue
+                    hop(block, way, step + 1, p).start()
+                    cross(block, *((0, CUT) if step == 0 and p == 0 else carried(step, way, 0)[p]))
+                for way in range(2):
+                    if step == far - 2 and holds_lent(way, p):
+                        pl.when(core == 1)(
+                            functools.partial(lend, block_at(step + 1, way), way, p)
+                        )
+                    if LENT and step == far - 1 and p == len(carried(step, way, 0)) - 1:
+                        lent_arrive(block_at(step + 1, way), way)
 
         def drain(sem, count):
             some = gathered.at[pl.ds(0, count), :]
             pltpu.make_async_copy(some, some, sem).wait()
 
-        drain(d2d_recv, rings * rows)
-        drain(ici_send, (rings - 1) * rows - 2 * EARLY)
-        drain(d2d_send, rings * rows)
+        def finish(side):
+            lent = 2 * LENT
+            drain(d2d_recv, rings * rows - (lent + 2 * CUT if side == 1 and LENT else 0))
+            drain(ici_send, (rings - 1) * rows - 2 * EARLY + (2 * lent if side == 1 else -lent))
+            drain(d2d_send, rings * rows - (lent if side == 0 else 0))
+
+        each_side(finish)
         pltpu.make_async_copy(others, others, peak_send).wait()
         if EARLY:
             pltpu.make_async_copy(early, early, early_send).wait()
@@ -233,7 +297,7 @@
             pltpu.VMEM((n, 1, total), jnp.float32),
             pltpu.VMEM((2, max(EARLY, 8), total), jnp.float32),
             pltpu.SemaphoreType.DMA((LOADS,)),
-            pltpu.SemaphoreType.DMA((9,)),
+            pltpu.SemaphoreType.DMA((13,)),
             pltpu.SemaphoreType.DMA((slots,)),
         ],
         compiler_params=pltpu.CompilerParams(

time: 80.7 us -> 80.1 us (level)
  no operation moved by 1% of the time
where the time goes in v3:
time: 80.1 us; the launch traced here: 80 us
  Pallas kernels  79.3 us (99%)
    pallas_call x1, Pallas kernels, body(): held = make_kernel(n, rows, widths)(*ins)  74.7 us
    pallas_call x1, Pallas kernels, body(): pl.pallas_call(put_out, name='put_out', out_shape=tuple((jax.ShapeDtypeSt...  4.65 us

profile of v3, /device:TPU:1, one launch (start us, length us, event | category | flops | bytes accessed | tf_op | source)
XLA Modules:
  0.0 80.0 jit_solution(8267784796559803222)
XLA Ops:
  0.6 74.7 %update_gather.1 = (bf16[4096,1536]{1,0:T(8,128)(2,1)S(1)}, f32[1,1024]{1,0:T(1,128)S(1)}, f32[1,256]{1,0:T(1,128)S(1)}, f32[1,256]{1,0:T(1,128)S(1)}) custom-call(f32[256,1024]{1,0:T(8,128)} %refs_0_.1, f32[256,1024]{1,0:T(8,128)} %refs_1_.1, f32[256,1024]{1,0:T(8,128)} %refs_2_.1, f32[256,256]{1,0:T(8,128)} %refs_3_.1, f32[256,256]{1,0:T(8,128)} %refs_4_.1, ...), custom_call_target="tpu_custom_call" | custom-call | tf_op jit(solution)/shard_map/update_gather/pallas_call | solution.py:359
  75.3 4.7 %put_out.1 = (bf16[4096,1024]{1,0:T(8,128)(2,1)}, bf16[4096,256]{1,0:T(8,128)(2,1)}, bf16[4096,256]{1,0:T(8,128)(2,1)}, f32[1,1024]{1,0:T(1,128)}, f32[1,256]{1,0:T(1,128)}, /*index=5*/f32[1,256]{1,0:T(1,128)}) custom-call(bf16[4096,1536]{1,0:T(8,128)(2,1)S(1)} %get-tuple-element.16.gathered, f32[1,1024]{1,0:T(1,128)S(1)} %get-tuple-element.17.refs_0_, ...), custom_call_target="tpu_custom_call" | custom-call | tf_op jit(solution)/shard_map/put_out/pallas_call | solution.py:360

commit v4 on v3

--- a/solution.py
+++ b/solution.py
@@ -126,10 +126,10 @@
                 device_id_type=MESH,
             ).start()
 
-        def early_copy(way):
+        def early_copy(way, first=0, count=EARLY):
             return pltpu.make_async_remote_copy(
-                src_ref=fresh.at[pl.ds(0, EARLY), :],
-                dst_ref=early.at[way],
+                src_ref=fresh.at[pl.ds(first, count), :],
+                dst_ref=early.at[way, pl.ds(first, count), :],
                 send_sem=early_send,
                 recv_sem=one_sem.at[7 + way],
                 device_id={AXIS: ahead[way] * 2 + core},
@@ -137,8 +137,9 @@
             )
 
         if EARLY:
-            for way in range(2):
-                early_copy(way).start()
+            for first in range(0, EARLY, STRIP // 2):
+                for way in range(2):
+                    early_copy(way, first, STRIP // 2).start()
 
         others = peaks.at[pl.ds(0, n - 1)]
         pltpu.make_async_copy(others, others, peak_recv).wait()

time: 80.1 us -> 80.1 us (level)
  no operation moved by 1% of the time
where the time goes in v4:
time: 80.1 us; the launch traced here: 80 us
  Pallas kernels  79.3 us (99%)
    pallas_call x1, Pallas kernels, body(): held = make_kernel(n, rows, widths)(*ins)  74.7 us
    pallas_call x1, Pallas kernels, body(): pl.pallas_call(put_out, name='put_out', out_shape=tuple((jax.ShapeDtypeSt...  4.65 us

profile of v4, /device:TPU:1, one launch (start us, length us, event | category | flops | bytes accessed | tf_op | source)
XLA Modules:
  0.0 80.0 jit_solution(1909577119885618656)
XLA Ops:
  0.6 74.7 %update_gather.1 = (bf16[4096,1536]{1,0:T(8,128)(2,1)S(1)}, f32[1,1024]{1,0:T(1,128)S(1)}, f32[1,256]{1,0:T(1,128)S(1)}, f32[1,256]{1,0:T(1,128)S(1)}) custom-call(f32[256,1024]{1,0:T(8,128)} %refs_0_.1, f32[256,1024]{1,0:T(8,128)} %refs_1_.1, f32[256,1024]{1,0:T(8,128)} %refs_2_.1, f32[256,256]{1,0:T(8,128)} %refs_3_.1, f32[256,256]{1,0:T(8,128)} %refs_4_.1, ...), custom_call_target="tpu_custom_call" | custom-call | tf_op jit(solution)/shard_map/update_gather/pallas_call | solution.py:360
  75.3 4.7 %put_out.1 = (bf16[4096,1024]{1,0:T(8,128)(2,1)}, bf16[4096,256]{1,0:T(8,128)(2,1)}, bf16[4096,256]{1,0:T(8,128)(2,1)}, f32[1,1024]{1,0:T(1,128)}, f32[1,256]{1,0:T(1,128)}, /*index=5*/f32[1,256]{1,0:T(1,128)}) custom-call(bf16[4096,1536]{1,0:T(8,128)(2,1)S(1)} %get-tuple-element.16.gathered, f32[1,1024]{1,0:T(1,128)S(1)} %get-tuple-element.17.refs_0_, ...), custom_call_target="tpu_custom_call" | custom-call | tf_op jit(solution)/shard_map/put_out/pallas_call | solution.py:361
